TPU v7x, 256 devices: a whole 4x4x8 slice. The times are simulated.
256 devices in a mesh: seq: 32 (over y, z), head: 8 (over x, core).
Axes of the slice: x: 4, y: 4, z: 8, core: 2. Of those that a mesh axis runs over, the one named last changes fastest.
Arguments:
- tokens: bfloat16 [2, 4096, 2560], P(None, 'seq', 'head'), may hold values from -6 to 6
- token_mix: float32 [5, 2560], replicated, may hold values from 0.05 to 0.95
- receptance: bfloat16 [2560, 2560], P(None, 'head'), may hold values from -0.125 to 0.125
- key_weight: bfloat16 [2560, 2560], P(None, 'head'), may hold values from -0.125 to 0.125
- value_weight: bfloat16 [2560, 2560], P(None, 'head'), may hold values from -0.125 to 0.125
- decay_base: float32 [2560], P('head'), may hold values from -12.5 to -1.9
- decay_down_matrix: bfloat16 [2560, 96], replicated, may hold values from -0.125 to 0.125
- decay_up_matrix: bfloat16 [96, 2560], P(None, 'head'), may hold values from -0.625 to 0.625
- learn_base: float32 [2560], P('head'), may hold values from -1.5 to 1.5
- learning_down_matrix: bfloat16 [2560, 96], replicated, may hold values from -0.125 to 0.125
- learning_up_matrix: bfloat16 [96, 2560], P(None, 'head'), may hold values from -0.625 to 0.625
- key_scale: float32 [2560], P('head'), may hold values from 0.25 to 1.75
- key_blend: float32 [2560], P('head'), may hold values from 0.2 to 1
- norm_gain: float32 [2560], P('head'), may hold values from 0.25 to 1.75
- norm_bias: float32 [2560], P('head'), may hold values from -3 to 3
- output_weight: bfloat16 [2560, 2560], P('head'), may hold values from -0.125 to 0.125
Outputs:
- mixed_out: bfloat16 [2, 4096, 2560], P(None, 'seq', 'head')
All inputs are finite; a program needn't handle non-finite values.
Results may differ from a plain program's by a relative error of at most 0.014.
Values may be sent and summed in bfloat16 or wider, within the bound.
No kernel may reach another device: no remote copies, remote signals or barrier semaphores. Data moves between devices by JAX's collectives and lax.ppermute only.
A program may use at most 128 MiB of HBM per device.

v0:
```python
import jax
import jax.numpy as jnp
from jax import lax
from jax.sharding import Mesh
from jax.sharding import PartitionSpec as P

HEAD_SIZE = 64
SPAN = 64
SEQ = ("seq_0", "seq_1")


def shifted(block, axis, distance):
    devices = range(lax.axis_size(axis))
    route = [(i - distance, i) for i in devices if i - distance in devices]
    return lax.ppermute(block, axis, route)


def gather_turned(arrays, axis, dims):
    turned = [jnp.moveaxis(a, dim, 0) for a, dim in zip(arrays, dims)]
    widths = [t[0].size for t in turned]
    both = jnp.concatenate([t.reshape(-1, w) for t, w in zip(turned, widths)], axis=1)
    out = lax.all_gather(both, axis, axis=0, tiled=True)
    tiles = jnp.split(out, [sum(widths[:k]) for k in range(1, len(widths))], axis=1)
    return tuple(
        (
            jnp.moveaxis(b.reshape(-1, *t.shape[1:]), 0, dim)
            for b, t, dim in zip(tiles, turned, dims)
        )
    )


def filled_with(value, identity):
    return jnp.broadcast_to(jnp.asarray(identity, value.dtype), value.shape)


def prefix_by_axis(value, axes, combine, identity):
    before = start = filled_with(value, identity)
    running = value
    for axis in reversed(axes):
        length, position = (lax.axis_size(axis), lax.axis_index(axis))
        pieces = lax.all_gather(running, axis)
        inside, running = (start, start)
        for k in range(length):
            passed = k < position
            running = combine(running, pieces[k])
            inside = jnp.where(passed, running, inside)
        before = combine(inside, before)
    return before


def joined_along(tiles, dim):
    dims = list(tiles.shape[1:])
    dims[dim] *= tiles.shape[0]
    return jnp.moveaxis(tiles, 0, dim).reshape(dims)


def from_everyone(value, axis):
    copies = jnp.broadcast_to(value, (lax.axis_size(axis), *value.shape))
    return lax.all_to_all(copies, axis, split_axis=0, concat_axis=0, tiled=True)


def gather_directly(value, axis, dim):
    return joined_along(from_everyone(value, axis), dim)


def matmul(left, right):
    return jnp.matmul(left, right)


def combine_maps(earlier, later):
    size = later.shape[-2]
    moving = later[..., size:]
    adding = later[..., :size]
    return matmul(moving, earlier) + jnp.concatenate([adding, jnp.zeros_like(adding)], axis=-1)


def lower_pairs(first, second, keep):
    products = jnp.einsum("abcti,abcsi->abcts", first, second)
    return jnp.where(keep, products, 0.0)


def body(
    tokens,
    token_mix,
    receptance,
    key_weight,
    value_weight,
    decay_base,
    decay_down_matrix,
    decay_up_matrix,
    learn_base,
    learning_down_matrix,
    learning_up_matrix,
    key_scale,
    key_blend,
    norm_gain,
    norm_bias,
    output_weight,
):
    seq_count, length, local_width = tokens.shape
    row_count = seq_count * length
    head_count = local_width // HEAD_SIZE
    boundary = shifted(tokens[:, length - 1 :, :], SEQ, 1)
    weights = (receptance, decay_down_matrix, key_weight, value_weight, learning_down_matrix)
    feature_piece, edge_piece = gather_turned((tokens, boundary), "head", (2, 2))
    extent = feature_piece.shape[2]
    current = feature_piece.astype(jnp.float32)
    earlier = jnp.concatenate([edge_piece, feature_piece[:, :-1, :]], axis=1).astype(jnp.float32)
    change = earlier - current
    result = []
    for term_index in range(5):
        blended = (
            (current + change * token_mix[term_index])
            .astype(jnp.bfloat16)
            .reshape(row_count, extent)
        )
        weight_rows = weights[term_index]
        result.append(jnp.dot(blended, weight_rows, preferred_element_type=jnp.float32))
    recept_out, decay_pre, key_raw, value_out, learn_pre = tuple(result)
    decay_hidden = jnp.tanh(decay_pre).astype(jnp.bfloat16)
    learn_hidden = learn_pre.astype(jnp.bfloat16)
    decay_arg = decay_base + jnp.dot(
        decay_hidden, decay_up_matrix, preferred_element_type=jnp.float32
    )
    log_decay = -jnp.exp(-jax.nn.softplus(-decay_arg) - 0.5)
    learn_rate = jax.nn.sigmoid(
        learn_base + jnp.dot(learn_hidden, learning_up_matrix, preferred_element_type=jnp.float32)
    )
    scaled = (key_raw * key_scale).reshape(row_count, head_count, HEAD_SIZE)
    unit_key = (
        scaled / jnp.sqrt(jnp.sum(scaled * scaled, axis=-1, keepdims=True) + 1e-06)
    ).reshape(row_count, local_width)
    key_final = key_raw * (1.0 + (learn_rate - 1.0) * key_blend)
    span_count = length // SPAN

    def arrange(values):
        return values.reshape(seq_count, span_count, SPAN, head_count, HEAD_SIZE).transpose(
            0, 3, 1, 2, 4
        )

    recept_c = arrange(recept_out)
    decay_c = arrange(log_decay)
    unit_c = arrange(unit_key)
    learn_c = arrange(learn_rate)
    key_c = arrange(key_final)
    value_c = arrange(value_out)
    alpha_c = -unit_c
    beta_c = unit_c * learn_c
    cumul = jnp.cumsum(decay_c, axis=3)
    before_c = cumul - decay_c
    middle = cumul[:, :, :, SPAN // 2 - 1 : SPAN // 2, :]
    ending = cumul[:, :, :, SPAN - 1 :, :]
    left_alpha = alpha_c * jnp.exp(before_c - middle)
    left_recept = recept_c * jnp.exp(cumul - middle)
    right_beta = beta_c * jnp.exp(middle - cumul)
    right_key = key_c * jnp.exp(middle - cumul)
    positions = jnp.arange(SPAN)
    strict = positions[:, None] > positions[None, :]
    within = positions[:, None] >= positions[None, :]
    lower_ab = lower_pairs(left_alpha, right_beta, strict)
    lower_ak = lower_pairs(left_alpha, right_key, strict)
    lower_rb = lower_pairs(left_recept, right_beta, within)
    lower_rk = lower_pairs(left_recept, right_key, within)
    identity = jnp.eye(SPAN, dtype=jnp.float32)
    inverse = identity + lower_ab
    power = lower_ab
    for level in range(SPAN.bit_length() - 2):
        power = matmul(power, power)
        inverse = inverse + matmul(power, inverse)
    gain_key = matmul(inverse, alpha_c * jnp.exp(before_c))
    gain_value = matmul(inverse, matmul(lower_ak, value_c))
    query_eff = recept_c * jnp.exp(cumul) + matmul(lower_rb, gain_key)
    local_out = matmul(lower_rb, gain_value) + matmul(lower_rk, value_c)
    beta_end = beta_c * jnp.exp(ending - cumul)
    key_end = key_c * jnp.exp(ending - cumul)
    head_eye = jnp.eye(HEAD_SIZE, dtype=jnp.float32)
    transition = jnp.einsum("abctj,abctk->abcjk", beta_end, gain_key)
    transition = transition + head_eye * jnp.swapaxes(jnp.exp(ending), -1, -2)
    increment = jnp.einsum("abctk,abctv->abckv", beta_end, gain_value)
    increment = increment + jnp.einsum("abctk,abctv->abckv", key_end, value_c)
    start_aug = jnp.broadcast_to(
        jnp.concatenate([jnp.zeros((HEAD_SIZE, HEAD_SIZE), jnp.float32), head_eye], axis=1),
        (seq_count, head_count, HEAD_SIZE, 2 * HEAD_SIZE),
    )

    def advance(carry, step_items):
        moving, adding = step_items
        following = matmul(moving, carry) + jnp.concatenate(
            [adding, jnp.zeros_like(adding)], axis=-1
        )
        return (following, carry)

    total, entries = lax.scan(
        advance, start_aug, (jnp.moveaxis(transition, 2, 0), jnp.moveaxis(increment, 2, 0))
    )
    prefix = prefix_by_axis(total, SEQ, combine_maps, start_aug)
    state_in = prefix[..., :HEAD_SIZE]
    span_state = entries[..., :HEAD_SIZE] + matmul(entries[..., HEAD_SIZE:], state_in)
    span_state = jnp.moveaxis(span_state, 0, 2)
    output_c = matmul(query_eff, span_state) + local_out
    wkv = output_c.transpose(0, 2, 3, 1, 4).reshape(row_count, head_count, HEAD_SIZE)
    centred = wkv - jnp.mean(wkv, axis=-1, keepdims=True)
    spread = jnp.mean(centred * centred, axis=-1, keepdims=True)
    normed = (centred / jnp.sqrt(spread + 0.00064)).reshape(
        row_count, local_width
    ) * norm_gain + norm_bias
    normed = normed.astype(jnp.bfloat16)
    own_columns = lax.all_to_all(output_weight, "head", split_axis=1, concat_axis=0, tiled=True)
    weight_rows = own_columns
    result = jnp.dot(
        gather_directly(normed, "head", 1), weight_rows, preferred_element_type=jnp.float32
    )
    return result.astype(jnp.bfloat16).reshape(seq_count, length, local_width)


def solution(mesh):
    torus = Mesh(mesh.devices.reshape(4, 8, mesh.shape["head"]), ("seq_0", "seq_1", "head"))
    placed = (
        P(None, SEQ, "head"),
        P(),
        P(None, "head"),
        P(None, "head"),
        P(None, "head"),
        P("head"),
        P(),
        P(None, "head"),
        P("head"),
        P(),
        P(None, "head"),
        P("head"),
        P("head"),
        P("head"),
        P("head"),
        P("head", None),
    )
    return jax.shard_map(
        body, mesh=torus, in_specs=placed, out_specs=P(None, SEQ, "head"), check_vma=False
    )
```

profile of v0, /device:TPU:1, one launch (start us, length us, event | category | flops | bytes accessed | tf_op | source)
XLA Modules:
  0.0 227.0 jit_solution(18370085318308386240)
XLA Ops:
  7.7 4.4 %collective-permute-start = (bf16[2,1,320]{1,2,0:T(8,128)(2,1)S(1)}, bf16[2,1,320]{1,2,0:T(8,128)(2,1)S(1)}, u32[]{:S(2)}, u32[]{:S(2)}) collective-permute-start(bf16[2,1,320]{1,2,0:T(8,128)(2,1)S(1)} %slice.141), channel_id=1, source_target_pairs={{0,8},{8,16},{16,24},{24,32},{32,40},{40,48},{48,56},{56,64},{64,7... | collective-permute-start | bytes 3848 | tf_op jit(solution)/shard_map/ppermute | solution.py:15
  13.0 1.9 collective-permute-done
  14.9 2.0 copy.177
  18.1 32.8 %all-gather.11.cloned.1.call-done = bf16[8,320,258]{1,2,0:T(8,128)(2,1)} async-done(((bf16[1,320,258]{1,2,0:T(8,128)(2,1)}), bf16[8,320,258]{1,2,0:T(8,128)(2,1)}) %all-gather.11.cloned.1.call-update) | async-done | bytes 1320976 | tf_op jit(solution)/shard_map/all_gather | solution.py:22
  52.5 2.4 %reshape.160 = bf16[2560,258]{0,1:T(8,128)(2,1)} reshape(bf16[8,320,258]{1,0,2:T(8,128)(2,1)S(1)} %copy.125) | data formatting | bytes 2641920
  57.2 3.4 %fusion.3 = (bf16[2,128,2560]{2,1,0:T(8,128)(2,1)}, bf16[2,128,2560]{2,1,0:T(8,128)(2,1)S(1)}, bf16[2,128,2560]{2,1,0:T(8,128)(2,1)}, bf16[2,128,2560]{2,1,0:T(8,128)(2,1)}, bf16[2,128,2560]{2,1,0:T(8,128)(2,1)}) fusion(bf16[2,128,2560]{2,1,0:T(8,128)(2,1)S(1)} %bitcast.218, f32[2560]{0:T(1024)S(1)} %get-tuple-element.55, ...), kind=kLoop, calls=%fused_computation.12 | loop fusion | flops 13762560 | bytes 9226240 | tf_op jit(solution)/shard_map/convert_element_type | solution.py:114
  60.5 2.0 fusion.75
  65.5 2.3 %fusion.32 = f32[256,320]{0,1:T(8,128)S(1)} fusion(bf16[96,320]{1,0:T(8,128)(2,1)S(1)} %copy-done.39, bf16[256,2560]{1,0:T(8,128)(2,1)} %bitcast.226, bf16[2560,96]{0,1:T(8,128)(2,1)} %param.27, f32[320]{0:T(512)S(1)} %copy-done.41), kind=kOutput, calls=%fused_computation.66 | convolution fusion | flops 141910016 | bytes 2192640 | tf_op jit(solution)/shard_map/dot_general | solution.py:127
  69.1 3.0 %fusion.134 = (f32[256,320]{0,1:T(8,128)S(1)}, f32[256,320]{0,1:T(8,128)}, f32[256,320]{0,1:T(8,128)}) fusion(f32[320]{0:T(512)S(1)} %copy-done.34, f32[320]{0:T(512)S(1)} %copy-done.35, f32[256,320]{0,1:T(8,128)} %copy-done.9, bf16[256,2560]{1,0:T(8,128)(2,1)S(1)} %bitcast.221, bf16[2560,320]{0,1:T(8,128)(2,1)} %param.21), kind=kOutput, calls=%fused_computation.205 | convolution fusion | flops 419921920 | bytes 4262400 | tf_op jit(solution)/shard_map/dot_general | solution.py:118
  76.7 1.7 reduce_window_sum.11
  79.7 4.9 %bitcast_multiply_fusion = (bf16[2,5,2,64,64]{4,3,1,2,0:T(8,128)(2,1)}, bf16[2,5,2,64,64]{4,3,1,2,0:T(8,128)(2,1)S(1)}, bf16[2,5,2,64,64]{4,3,1,2,0:T(8,128)(2,1...) fusion(f32[2,2,64,5,64]{4,2,3,1,0:T(8,128)} %copy.147, ...), kind=kOutput, calls=%fused_computation.78 | convolution fusion | flops 421232640 | bytes 6077440 | tf_op jit(solution)/shard_map/dot_general | solution.py:118
  88.2 3.1 %convolution_bitcast_fusion.2 = bf16[2,5,2,64,64]{4,3,1,2,0:T(8,128)(2,1)S(1)} fusion(bf16[2,2,64,2560,1]{3,2,4,1,0:T(8,128)(2,1)} %bitcast.224, bf16[5,64,2560,1,1]{2,1,0,4,3:T(8,128)(2,1)} %bitcast.235), kind=kOutput, calls=%fused_computation.39 | convolution fusion | flops 419430400 | bytes 3112960 | tf_op jit(solution)/shard_map/dot_general | solution.py:118
  95.8 2.4 %while.12 = (s32[]{:T(128)}, f32[2,5,64,128]{3,2,1,0:T(8,128)S(1)}, f32[2,2,5,64,128]{4,3,2,1,0:T(8,128)}, bf16[2,2,5,64,64]{4,3,0,2,1:T(8,128)(2,1)}, f32[2,2,5,64,64]{4,3,0,2,1:T(8,128)S(1)}, /*index=5*/s32[]{:T(128)}) while((s32[]{:T(128)}, f32[2,5,64,128]{3,2,1,0:T(8,128)S(1)}, f32[2,2,5,64,128]{4,3,2,1,0:T(8,128)}, ...), condition=%wide.region_3.4_spmd, body=%wide.region_2.3_spmd.sunk | while | flops 10567682 | bytes 3441257 | solution.py:193
  99.2 38.7 %all-gather.7.cloned.1.call-done = f32[16,5,64,128]{3,2,1,0:T(8,128)} async-done(((f32[2,5,64,128]{3,2,1,0:T(8,128)}), f32[16,5,64,128]{3,2,1,0:T(8,128)}) %all-gather.7.cloned.1.call-update) | async-done | bytes 2621456 | tf_op jit(solution)/shard_map/all_gather | solution.py:41
  151.1 2.0 convolution_add_fusion.14
  153.2 3.8 %copy.165 = bf16[320,2560]{0,1:T(8,128)(2,1)} copy(bf16[320,2560]{1,0:T(8,128)(2,1)} %param.33) | data formatting | bytes 3276800 | tf_op args[15]
  157.0 8.1 %all-to-all-start.1 = ((bf16[320,8,320]{0,2,1:T(8,128)(2,1)}), bf16[320,8,320]{0,2,1:T(8,128)(2,1)}, u32[]{:S(2)}, u32[]{:S(2)}) async-start(bf16[320,8,320]{0,2,1:T(8,128)(2,1)} %bitcast.220), calls=%async_computation.1 | async-start | bytes 3932160 | tf_op jit(solution)/shard_map/all_to_all | solution.py:208
  167.9 2.0 convolution_add_fusion.8
  170.3 11.1 %all-gather.9.cloned.1.call-done = f32[8,5,64,128]{3,2,1,0:T(8,128)} async-done(((f32[2,5,64,128]{3,2,1,0:T(8,128)}), f32[8,5,64,128]{3,2,1,0:T(8,128)}) %all-gather.9.cloned.1.call-update) | async-done | bytes 1310736 | tf_op jit(solution)/shard_map/all_gather | solution.py:41
  185.3 2.2 fusion.28
  187.6 1.8 fusion.12
  190.6 1.8 fusion.135
  194.1 23.6 %all_to_all.21 = bf16[8,256,320]{1,2,0:T(8,128)(2,1)S(1)} all-to-all(bf16[8,256,320]{1,2,0:T(8,128)(2,1)S(1)} %broadcast_in_dim.60), channel_id=1, replica_groups=mesh['seq_0'=4,'seq_1'=8,'head'=8] {'head'}, dimensions={0} | all-to-all | bytes 2621440 | tf_op jit(solution)/shard_map/all_to_all | solution.py:59
  217.7 2.1 fusion.39
  (176 shorter events, 52.1 us)
Async XLA Ops:
  6.5 73.2 %copy-start = (bf16[2560,320]{0,1:T(8,128)(2,1)S(1)}, bf16[2560,320]{0,1:T(8,128)(2,1)}, u32[]{:S(2)}) copy-start(bf16[2560,320]{0,1:T(8,128)(2,1)} %param.20) | copy-start | bytes 4915204
  6.5 11.5 %copy-start.33 = (f32[5,2560]{1,0:T(8,128)S(1)}, f32[5,2560]{1,0:T(8,128)}, u32[]{:S(2)}) copy-start(f32[5,2560]{1,0:T(8,128)} %param.19) | copy-start | bytes 153604
  6.5 44.4 %all-gather.11.cloned.1.call-start = ((), (), s32[]{:S(2)}) async-start(), calls=%async_computation.4 | async-start | bytes 1824768 | tf_op jit(solution)/shard_map/all_gather | solution.py:22
  7.7 7.2 %collective-permute-start = (bf16[2,1,320]{1,2,0:T(8,128)(2,1)S(1)}, bf16[2,1,320]{1,2,0:T(8,128)(2,1)S(1)}, u32[]{:S(2)}, u32[]{:S(2)}) collective-permute-start(bf16[2,1,320]{1,2,0:T(8,128)(2,1)S(1)} %slice.141), channel_id=1, source_target_pairs={{0,8},{8,16},{16,24},{24,32},{32,40},{40,48},{48,56},{56,64},{64,7... | collective-permute-start | bytes 3848 | tf_op jit(solution)/shard_map/ppermute | solution.py:15
  17.8 120.0 %all-gather.7.cloned.1.call-start = ((), (), s32[]{:S(2)}) async-start(), calls=%async_computation.2 | async-start | bytes 2949120 | tf_op jit(solution)/shard_map/all_gather | solution.py:41
  57.1 3.4 %copy-start.38 = (bf16[96,320]{1,0:T(8,128)(2,1)S(1)}, bf16[96,320]{1,0:T(8,128)(2,1)}, u32[]{:S(2)}) copy-start(bf16[96,320]{1,0:T(8,128)(2,1)} %param.25) | copy-start | bytes 184324
  57.1 3.4 %copy-start.40 = (f32[320]{0:T(512)S(1)}, f32[320]{0:T(512)}, u32[]{:S(2)}) copy-start(f32[320]{0:T(512)} %param.23) | copy-start | bytes 3844
  65.5 3.6 %copy-start.2 = (bf16[2,128,2560]{2,1,0:T(8,128)(2,1)S(1)}, bf16[2,128,2560]{2,1,0:T(8,128)(2,1)}, u32[]{:S(2)}) copy-start(bf16[2,128,2560]{2,1,0:T(8,128)(2,1)} %get-tuple-element.74) | copy-start | bytes 3932164
  65.5 3.6 %copy-start.34 = (f32[320]{0:T(512)S(1)}, f32[320]{0:T(512)}, u32[]{:S(2)}) copy-start(f32[320]{0:T(512)} %param.29) | copy-start | bytes 3844
  65.5 3.6 %copy-start.35 = (f32[320]{0:T(512)S(1)}, f32[320]{0:T(512)}, u32[]{:S(2)}) copy-start(f32[320]{0:T(512)} %param.30) | copy-start | bytes 3844
  75.2 3.2 %copy-start.6 = (f32[2,2,64,5,64]{2,1,0,4,3:T(2,128)S(1)}, f32[2,2,64,5,64]{2,1,0,4,3:T(2,128)}, u32[]{:S(2)}) copy-start(f32[2,2,64,5,64]{2,1,0,4,3:T(2,128)} %reshape.129) | copy-start | bytes 983044
  78.3 6.2 %copy-start.3 = (f32[2,5,2,64,64]{4,3,2,1,0:T(8,128)}, f32[2,5,2,64,64]{4,3,2,1,0:T(8,128)S(1)}, u32[]{:S(2)}) copy-start(f32[2,5,2,64,64]{4,3,2,1,0:T(8,128)S(1)} %reduce_window_sum.11) | copy-start | bytes 983044
  95.8 42.1 %copy-start.32 = (pred[128]{0:T(512)(128)(4,1)S(1)}, pred[128]{0:T(512)(128)(4,1)}, u32[]{:S(2)}) copy-start(pred[128]{0:T(512)(128)(4,1)} %constant.67.clone.1) | copy-start | bytes 388
  98.9 82.4 %all-gather.9.cloned.1.call-start = ((), (), s32[]{:S(2)}) async-start(), calls=%async_computation.3 | async-start | bytes 1638400 | tf_op jit(solution)/shard_map/all_gather | solution.py:41
  157.0 37.0 %all-to-all-start.1 = ((bf16[320,8,320]{0,2,1:T(8,128)(2,1)}), bf16[320,8,320]{0,2,1:T(8,128)(2,1)}, u32[]{:S(2)}, u32[]{:S(2)}) async-start(bf16[320,8,320]{0,2,1:T(8,128)(2,1)} %bitcast.220), calls=%async_computation.1 | async-start | bytes 3932160 | tf_op jit(solution)/shard_map/all_to_all | solution.py:208
  166.6 3.2 %copy-start.12 = (f32[2,5,64,128]{3,2,1,0:T(8,128)S(1)}, f32[2,5,64,128]{3,2,1,0:T(8,128)}, u32[]{:S(2)}) copy-start(f32[2,5,64,128]{3,2,1,0:T(8,128)} %convolution_add_fusion.14) | copy-start | bytes 983044
  166.7 3.2 %copy-start.15 = (bf16[2,5,64,128]{3,2,1,0:T(8,128)(2,1)S(1)}, bf16[2,5,64,128]{3,2,1,0:T(8,128)(2,1)}, u32[]{:S(2)}) copy-start(bf16[2,5,64,128]{3,2,1,0:T(8,128)(2,1)} %copy-done.14) | copy-start | bytes 491524
  166.7 3.2 %copy-start.17 = (bf16[2,5,64,128]{3,2,1,0:T(8,128)(2,1)S(1)}, bf16[2,5,64,128]{3,2,1,0:T(8,128)(2,1)}, u32[]{:S(2)}) copy-start(bf16[2,5,64,128]{3,2,1,0:T(8,128)(2,1)} %copy-done.16) | copy-start | bytes 491524
  166.7 3.2 %copy-start.19 = (bf16[2,5,64,128]{3,2,1,0:T(8,128)(2,1)S(1)}, bf16[2,5,64,128]{3,2,1,0:T(8,128)(2,1)}, u32[]{:S(2)}) copy-start(bf16[2,5,64,128]{3,2,1,0:T(8,128)(2,1)} %copy-done.18) | copy-start | bytes 491524
  166.7 3.2 %copy-start.21 = (bf16[2,5,64,128]{3,2,1,0:T(8,128)(2,1)S(1)}, bf16[2,5,64,128]{3,2,1,0:T(8,128)(2,1)}, u32[]{:S(2)}) copy-start(bf16[2,5,64,128]{3,2,1,0:T(8,128)(2,1)} %copy-done.20) | copy-start | bytes 491524
  166.7 3.2 %copy-start.23 = (bf16[2,5,64,128]{3,2,1,0:T(8,128)(2,1)S(1)}, bf16[2,5,64,128]{3,2,1,0:T(8,128)(2,1)}, u32[]{:S(2)}) copy-start(bf16[2,5,64,128]{3,2,1,0:T(8,128)(2,1)} %copy-done.22) | copy-start | bytes 491524
  166.7 3.2 %copy-start.31 = (bf16[2,5,64,128]{3,2,1,0:T(8,128)(2,1)S(1)}, bf16[2,5,64,128]{3,2,1,0:T(8,128)(2,1)}, u32[]{:S(2)}) copy-start(bf16[2,5,64,128]{3,2,1,0:T(8,128)(2,1)} %copy-done.30) | copy-start | bytes 491524
  170.2 15.1 %copy-start.29 = (f32[2,5,64,128]{3,2,1,0:T(8,128)}, f32[2,5,64,128]{3,2,1,0:T(8,128)S(1)}, u32[]{:S(2)}) copy-start(f32[2,5,64,128]{3,2,1,0:T(8,128)S(1)} %convolution_add_fusion.13) | copy-start | bytes 983044
  185.3 4.1 %copy-start.10 = (bf16[2,5,2,64,64]{4,3,1,2,0:T(8,128)(2,1)S(1)}, bf16[2,5,2,64,64]{4,3,1,2,0:T(8,128)(2,1)}, u32[]{:S(2)}) copy-start(bf16[2,5,2,64,64]{4,3,1,2,0:T(8,128)(2,1)} %convolution_add_fusion.8) | copy-start | bytes 491524
  (24 other events, 39.4 us)
Sparse Core Ops, SparseCore 0:
  17.9 32.9 all-gather.10
  99.0 38.7 all-gather.6
  153.3 27.9 all-gather.8
where the time goes:
time: 228 us; the launch traced here: 227 us
  waiting for transfers between devices  84.5 us (37%)
  matrix products  52.8 us (23%)
  local copies, waits for them, and re-layouts  34 us (15%)
  blocking collectives  23.6 us (10%)
  between operations  13.9 us (6%)
  starting transfers between devices  12.8 us (6%)
  other arithmetic  5.44 us (2%)
    all_gather x2, waiting for transfers between devices, prefix_by_axis(): pieces = lax.all_gather(running, axis)  49.7 us
    all_gather x1, waiting for transfers between devices, gather_turned(): out = lax.all_gather(both, axis, axis=0, tiled=True)  32.8 us
    dot_general x31, matrix products, matmul(): return jnp.matmul(left, right)  30 us
    all_to_all x1, blocking collectives, from_everyone(): return lax.all_to_all(copies, axis, split_axis=0, concat_axis=0, tiled=True)  23.6 us
    unnamed x84, local copies, waits for them, and re-layouts  11 us
    dot_general x3, matrix products, body(): jnp.dot(blended, weight_rows, preferred_element_type=jnp.float32)  10.9 us
    all_to_all x1, starting transfers between devices, body(): lax.all_to_all(output_weight, 'head', split_axis=1, concat_axis=0, tiled=...  8.09 us
    reshape x6, local copies, waits for them, and re-layouts, arrange(): values.reshape(seq_count, span_count, SPAN, head_count, HEAD_SIZE)  5.87 us
  transfers between devices with their start and end apart: 5, of which 4 were waited for; matrix products, arithmetic and copies ran while one was open for 10% of the time, Pallas kernels for 0%

commit v1 on v0

--- a/solution.py
+++ b/solution.py
@@ -19,7 +19,9 @@
     turned = [jnp.moveaxis(a, dim, 0) for a, dim in zip(arrays, dims)]
     widths = [t[0].size for t in turned]
     both = jnp.concatenate([t.reshape(-1, w) for t, w in zip(turned, widths)], axis=1)
-    out = lax.all_gather(both, axis, axis=0, tiled=True)
+    out = jnp.concatenate(
+        lax.all_to_all(jnp.stack([both] * lax.axis_size(axis)), axis, 0, 0), axis=0
+    )
     tiles = jnp.split(out, [sum(widths[:k]) for k in range(1, len(widths))], axis=1)
     return tuple(
         (

time: 228 us -> 221 us (0.969)
  waiting for transfers between devices: 84.5 us -> 77.7 us
  starting transfers between devices: 12.8 us -> 18.5 us
  local copies, waits for them, and re-layouts: 34 us -> 29.4 us
    all_gather x1 -> x0, waiting for transfers between devices: 32.8 us -> none  [gather_turned(): out = lax.all_gather(both, axis, axis=0, tiled=True)]
    all_to_all x0 -> x1, waiting for transfers between devices: none -> 20.9 us  [gather_turned(): lax.all_to_all(jnp.stack([both] * lax.axis_size(axis)), axis, 0, 0)]
    all_to_all x0 -> x1, starting transfers between devices: none -> 5.96 us  [gather_turned(): lax.all_to_all(jnp.stack([both] * lax.axis_size(axis)), axis, 0, 0)]
    unnamed x84 -> x85, local copies, waits for them, and re-layouts: 11 us -> 5.37 us
    all_gather x2, waiting for transfers between devices: 49.7 us -> 54.9 us  [prefix_by_axis(): pieces = lax.all_gather(running, axis)]
    reshape x0 -> x1, local copies, waits for them, and re-layouts: none -> 2.78 us  [gather_turned(): jnp.concatenate(lax.all_to_all(jnp.stack([both] * lax.axis_size(axis)), a...]
  transfers between devices with their start and end apart: 5 -> 5, of which waited for: 4 -> 4; matrix products, arithmetic and copies ran while one was open for 10% -> 9% of each run, Pallas kernels for 0% -> 0%
where the time goes in v1:
time: 221 us; the launch traced here: 220 us
  waiting for transfers between devices  77.7 us (35%)
  matrix products  51.1 us (23%)
  local copies, waits for them, and re-layouts  29.4 us (13%)
  blocking collectives  23.6 us (11%)
  starting transfers between devices  18.5 us (8%)
  between operations  14.3 us (6%)
  other arithmetic  5.26 us (2%)
    all_gather x2, waiting for transfers between devices, prefix_by_axis(): pieces = lax.all_gather(running, axis)  54.9 us
    dot_general x31, matrix products, matmul(): return jnp.matmul(left, right)  28.2 us
    all_to_all x1, blocking collectives, from_everyone(): return lax.all_to_all(copies, axis, split_axis=0, concat_axis=0, tiled=True)  23.6 us
    all_to_all x1, waiting for transfers between devices, gather_turned(): lax.all_to_all(jnp.stack([both] * lax.axis_size(axis)), axis, 0, 0)  20.9 us
    dot_general x3, matrix products, body(): jnp.dot(blended, weight_rows, preferred_element_type=jnp.float32)  10.9 us
    all_to_all x1, starting transfers between devices, body(): lax.all_to_all(output_weight, 'head', split_axis=1, concat_axis=0, tiled=...  8.11 us
    all_to_all x1, starting transfers between devices, gather_turned(): lax.all_to_all(jnp.stack([both] * lax.axis_size(axis)), axis, 0, 0)  5.96 us
    reshape x6, local copies, waits for them, and re-layouts, arrange(): values.reshape(seq_count, span_count, SPAN, head_count, HEAD_SIZE)  5.87 us
  transfers between devices with their start and end apart: 5, of which 4 were waited for; matrix products, arithmetic and copies ran while one was open for 9% of the time, Pallas kernels for 0%

profile of v1, /device:TPU:1, one launch (start us, length us, event | category | flops | bytes accessed | tf_op | source)
XLA Modules:
  0.0 219.9 jit_solution(7857282521917453723)
XLA Ops:
  7.7 4.4 %collective-permute-start = (bf16[2,1,320]{1,2,0:T(8,128)(2,1)S(1)}, bf16[2,1,320]{1,2,0:T(8,128)(2,1)S(1)}, u32[]{:S(2)}, u32[]{:S(2)}) collective-permute-start(bf16[2,1,320]{1,2,0:T(8,128)(2,1)S(1)} %slice.141), channel_id=1, source_target_pairs={{0,8},{8,16},{16,24},{24,32},{32,40},{40,48},{48,56},{56,64},{64,7... | collective-permute-start | bytes 3848 | tf_op jit(solution)/shard_map/ppermute | solution.py:15
  13.0 1.9 collective-permute-done
  14.9 2.0 copy.177
  18.5 6.0 %all-to-all-start = ((bf16[8,320,258]{1,2,0:T(8,128)(2,1)}), bf16[8,320,258]{1,2,0:T(8,128)(2,1)S(1)}, u32[]{:S(2)}, u32[]{:S(2)}) async-start(bf16[8,320,258]{1,2,0:T(8,128)(2,1)} %stack.2), calls=%async_computation | async-start | bytes 3244032 | tf_op jit(solution)/shard_map/all_to_all | solution.py:23
  24.7 20.9 %all-to-all-done = bf16[8,320,258]{1,2,0:T(8,128)(2,1)S(1)} async-done(((bf16[8,320,258]{1,2,0:T(8,128)(2,1)}), bf16[8,320,258]{1,2,0:T(8,128)(2,1)S(1)}, u32[]{:S(2)}, u32[]{:S(2)}) %all-to-all-start) | async-done | bytes 1320992 | tf_op jit(solution)/shard_map/all_to_all | solution.py:23
  46.9 2.8 %reshape.127 = bf16[2560,258]{0,1:T(8,128)(2,1)S(1)} reshape(bf16[8,320,258]{1,0,2:T(8,128)(2,1)} %copy.125) | data formatting | bytes 2641920 | tf_op jit(solution)/shard_map/reshape | solution.py:22
  49.9 3.2 %fusion.3 = (bf16[2,128,2560]{2,1,0:T(8,128)(2,1)}, bf16[2,128,2560]{2,1,0:T(8,128)(2,1)S(1)}, bf16[2,128,2560]{2,1,0:T(8,128)(2,1)}, bf16[2,128,2560]{2,1,0:T(8,128)(2,1)}, bf16[2,128,2560]{2,1,0:T(8,128)(2,1)}) fusion(bf16[2,128,2560]{2,1,0:T(8,128)(2,1)S(1)} %bitcast.217, f32[2560]{0:T(1024)S(1)} %get-tuple-element.55, ...), kind=kLoop, calls=%fused_computation.12 | loop fusion | flops 13762560 | bytes 9226240 | tf_op jit(solution)/shard_map/convert_element_type | solution.py:116
  53.1 2.0 fusion.75
  58.0 2.3 %fusion.32 = f32[256,320]{0,1:T(8,128)S(1)} fusion(bf16[96,320]{1,0:T(8,128)(2,1)S(1)} %copy-done.40, bf16[256,2560]{1,0:T(8,128)(2,1)} %bitcast.225, bf16[2560,96]{0,1:T(8,128)(2,1)} %param.27, f32[320]{0:T(512)S(1)} %copy-done.42), kind=kOutput, calls=%fused_computation.66 | convolution fusion | flops 141910016 | bytes 2192640 | tf_op jit(solution)/shard_map/dot_general | solution.py:129
  61.6 3.0 %fusion.134 = (f32[256,320]{0,1:T(8,128)S(1)}, f32[256,320]{0,1:T(8,128)}, f32[256,320]{0,1:T(8,128)}) fusion(f32[320]{0:T(512)S(1)} %copy-done.35, f32[320]{0:T(512)S(1)} %copy-done.36, f32[256,320]{0,1:T(8,128)} %copy-done.9, bf16[256,2560]{1,0:T(8,128)(2,1)S(1)} %bitcast.220, bf16[2560,320]{0,1:T(8,128)(2,1)} %param.21), kind=kOutput, calls=%fused_computation.205 | convolution fusion | flops 419921920 | bytes 4262400 | tf_op jit(solution)/shard_map/dot_general | solution.py:120
  69.2 1.7 reduce_window_sum.11
  72.2 4.9 %bitcast_multiply_fusion = (bf16[2,5,2,64,64]{4,3,1,2,0:T(8,128)(2,1)}, bf16[2,5,2,64,64]{4,3,1,2,0:T(8,128)(2,1)S(1)}, bf16[2,5,2,64,64]{4,3,1,2,0:T(8,128)(2,1...) fusion(f32[2,2,64,5,64]{4,2,3,1,0:T(8,128)} %copy.147, ...), kind=kOutput, calls=%fused_computation.78 | convolution fusion | flops 421232640 | bytes 6077440 | tf_op jit(solution)/shard_map/dot_general | solution.py:120
  80.8 3.1 %convolution_bitcast_fusion.2 = bf16[2,5,2,64,64]{4,3,1,2,0:T(8,128)(2,1)S(1)} fusion(bf16[2,2,64,2560,1]{3,2,4,1,0:T(8,128)(2,1)} %bitcast.223, bf16[5,64,2560,1,1]{2,1,0,4,3:T(8,128)(2,1)} %bitcast.233), kind=kOutput, calls=%fused_computation.39 | convolution fusion | flops 419430400 | bytes 3112960 | tf_op jit(solution)/shard_map/dot_general | solution.py:120
  88.0 2.4 %while.12 = (s32[]{:T(128)}, f32[2,5,64,128]{3,2,1,0:T(8,128)S(1)}, f32[2,2,5,64,128]{4,3,2,1,0:T(8,128)}, bf16[2,2,5,64,64]{4,3,0,2,1:T(8,128)(2,1)}, f32[2,2,5,64,64]{4,3,0,2,1:T(8,128)S(1)}, /*index=5*/s32[]{:T(128)}) while((s32[]{:T(128)}, f32[2,5,64,128]{3,2,1,0:T(8,128)S(1)}, f32[2,2,5,64,128]{4,3,2,1,0:T(8,128)}, ...), condition=%wide.region_3.4_spmd, body=%wide.region_2.3_spmd.sunk | while | flops 10567682 | bytes 3441257 | solution.py:195
  91.2 42.2 %all-gather.5.cloned.1.call-done = f32[16,5,64,128]{3,2,1,0:T(8,128)} async-done(((f32[2,5,64,128]{3,2,1,0:T(8,128)}), f32[16,5,64,128]{3,2,1,0:T(8,128)}) %all-gather.5.cloned.1.call-update) | async-done | bytes 2621456 | tf_op jit(solution)/shard_map/all_gather | solution.py:43
  143.7 2.1 convolution_add_fusion.14
  145.8 3.8 %copy.165 = bf16[320,2560]{0,1:T(8,128)(2,1)} copy(bf16[320,2560]{1,0:T(8,128)(2,1)} %param.33) | data formatting | bytes 3276800 | tf_op args[15]
  149.7 8.1 %all-to-all-start.2 = ((bf16[320,8,320]{0,2,1:T(8,128)(2,1)}), bf16[320,8,320]{0,2,1:T(8,128)(2,1)}, u32[]{:S(2)}, u32[]{:S(2)}) async-start(bf16[320,8,320]{0,2,1:T(8,128)(2,1)} %bitcast.219), calls=%async_computation.2 | async-start | bytes 3932160 | tf_op jit(solution)/shard_map/all_to_all | solution.py:210
  161.2 12.7 %all-gather.7.cloned.1.call-done = f32[8,5,64,128]{3,2,1,0:T(8,128)} async-done(((f32[2,5,64,128]{3,2,1,0:T(8,128)}), f32[8,5,64,128]{3,2,1,0:T(8,128)}) %all-gather.7.cloned.1.call-update) | async-done | bytes 1310736 | tf_op jit(solution)/shard_map/all_gather | solution.py:43
  177.9 2.2 fusion.28
  180.1 1.8 fusion.12
  183.1 1.8 fusion.135
  186.7 23.6 %all_to_all.26 = bf16[8,256,320]{1,2,0:T(8,128)(2,1)S(1)} all-to-all(bf16[8,256,320]{1,2,0:T(8,128)(2,1)S(1)} %broadcast_in_dim.60), channel_id=1, replica_groups=mesh['seq_0'=4,'seq_1'=8,'head'=8] {'head'}, dimensions={0} | all-to-all | bytes 2621440 | tf_op jit(solution)/shard_map/all_to_all | solution.py:61
  210.2 2.1 fusion.39
  (178 shorter events, 47.1 us)
Async XLA Ops:
  6.5 65.7 %copy-start = (bf16[2560,320]{0,1:T(8,128)(2,1)S(1)}, bf16[2560,320]{0,1:T(8,128)(2,1)}, u32[]{:S(2)}) copy-start(bf16[2560,320]{0,1:T(8,128)(2,1)} %param.20) | copy-start | bytes 4915204
  7.7 7.2 %collective-permute-start = (bf16[2,1,320]{1,2,0:T(8,128)(2,1)S(1)}, bf16[2,1,320]{1,2,0:T(8,128)(2,1)S(1)}, u32[]{:S(2)}, u32[]{:S(2)}) collective-permute-start(bf16[2,1,320]{1,2,0:T(8,128)(2,1)S(1)} %slice.141), channel_id=1, source_target_pairs={{0,8},{8,16},{16,24},{24,32},{32,40},{40,48},{48,56},{56,64},{64,7... | collective-permute-start | bytes 3848 | tf_op jit(solution)/shard_map/ppermute | solution.py:15
  18.5 6.1 %copy-start.34 = (f32[5,2560]{1,0:T(8,128)S(1)}, f32[5,2560]{1,0:T(8,128)}, u32[]{:S(2)}) copy-start(f32[5,2560]{1,0:T(8,128)} %param.19) | copy-start | bytes 153604
  18.5 27.1 %all-to-all-start = ((bf16[8,320,258]{1,2,0:T(8,128)(2,1)}), bf16[8,320,258]{1,2,0:T(8,128)(2,1)S(1)}, u32[]{:S(2)}, u32[]{:S(2)}) async-start(bf16[8,320,258]{1,2,0:T(8,128)(2,1)} %stack.2), calls=%async_computation | async-start | bytes 3244032 | tf_op jit(solution)/shard_map/all_to_all | solution.py:23
  24.4 109.0 %all-gather.5.cloned.1.call-start = ((), (), s32[]{:S(2)}) async-start(), calls=%async_computation.3 | async-start | bytes 2949120 | tf_op jit(solution)/shard_map/all_gather | solution.py:43
  49.8 3.2 %copy-start.39 = (bf16[96,320]{1,0:T(8,128)(2,1)S(1)}, bf16[96,320]{1,0:T(8,128)(2,1)}, u32[]{:S(2)}) copy-start(bf16[96,320]{1,0:T(8,128)(2,1)} %param.25) | copy-start | bytes 184324
  49.9 3.2 %copy-start.41 = (f32[320]{0:T(512)S(1)}, f32[320]{0:T(512)}, u32[]{:S(2)}) copy-start(f32[320]{0:T(512)} %param.23) | copy-start | bytes 3844
  58.0 3.6 %copy-start.2 = (bf16[2,128,2560]{2,1,0:T(8,128)(2,1)S(1)}, bf16[2,128,2560]{2,1,0:T(8,128)(2,1)}, u32[]{:S(2)}) copy-start(bf16[2,128,2560]{2,1,0:T(8,128)(2,1)} %get-tuple-element.74) | copy-start | bytes 3932164
  58.0 3.6 %copy-start.35 = (f32[320]{0:T(512)S(1)}, f32[320]{0:T(512)}, u32[]{:S(2)}) copy-start(f32[320]{0:T(512)} %param.29) | copy-start | bytes 3844
  58.0 3.6 %copy-start.36 = (f32[320]{0:T(512)S(1)}, f32[320]{0:T(512)}, u32[]{:S(2)}) copy-start(f32[320]{0:T(512)} %param.30) | copy-start | bytes 3844
  67.7 3.2 %copy-start.6 = (f32[2,2,64,5,64]{2,1,0,4,3:T(2,128)S(1)}, f32[2,2,64,5,64]{2,1,0,4,3:T(2,128)}, u32[]{:S(2)}) copy-start(f32[2,2,64,5,64]{2,1,0,4,3:T(2,128)} %reshape.135) | copy-start | bytes 983044
  70.9 6.2 %copy-start.3 = (f32[2,5,2,64,64]{4,3,2,1,0:T(8,128)}, f32[2,5,2,64,64]{4,3,2,1,0:T(8,128)S(1)}, u32[]{:S(2)}) copy-start(f32[2,5,2,64,64]{4,3,2,1,0:T(8,128)S(1)} %reduce_window_sum.11) | copy-start | bytes 983044
  80.7 3.1 %copy-start.29 = (bf16[2,5,2,64,64]{4,3,1,2,0:T(8,128)(2,1)S(1)}, bf16[2,5,2,64,64]{4,3,1,2,0:T(8,128)(2,1)}, u32[]{:S(2)}) copy-start(bf16[2,5,2,64,64]{4,3,1,2,0:T(8,128)(2,1)} %get-tuple-element.88) | copy-start | bytes 491524
  80.8 4.1 %copy-start.28 = (bf16[2,5,2,64,64]{4,3,2,1,0:T(8,128)(2,1)S(1)}, bf16[2,5,2,64,64]{4,3,2,1,0:T(8,128)(2,1)}, u32[]{:S(2)}) copy-start(bf16[2,5,2,64,64]{4,3,2,1,0:T(8,128)(2,1)} %convolution_select_fusion.1) | copy-start | bytes 491524
  88.0 45.4 %copy-start.33 = (pred[128]{0:T(512)(128)(4,1)S(1)}, pred[128]{0:T(512)(128)(4,1)}, u32[]{:S(2)}) copy-start(pred[128]{0:T(512)(128)(4,1)} %constant.67.clone.1) | copy-start | bytes 388
  91.1 82.8 %all-gather.7.cloned.1.call-start = ((), (), s32[]{:S(2)}) async-start(), calls=%async_computation.4 | async-start | bytes 1638400 | tf_op jit(solution)/shard_map/all_gather | solution.py:43
  138.1 7.7 %copy-start.14 = (bf16[2,5,64,128]{3,2,1,0:T(8,128)(2,1)}, bf16[2,5,64,128]{3,2,1,0:T(8,128)(2,1)S(1)}, u32[]{:S(2)}) copy-start(bf16[2,5,64,128]{3,2,1,0:T(8,128)(2,1)S(1)} %convolution_add_fusion.19) | copy-start | bytes 491524
  139.5 10.2 %copy-start.16 = (bf16[2,5,64,128]{3,2,1,0:T(8,128)(2,1)}, bf16[2,5,64,128]{3,2,1,0:T(8,128)(2,1)S(1)}, u32[]{:S(2)}) copy-start(bf16[2,5,64,128]{3,2,1,0:T(8,128)(2,1)S(1)} %convolution_add_fusion.18) | copy-start | bytes 491524
  140.9 8.8 %copy-start.18 = (bf16[2,5,64,128]{3,2,1,0:T(8,128)(2,1)}, bf16[2,5,64,128]{3,2,1,0:T(8,128)(2,1)S(1)}, u32[]{:S(2)}) copy-start(bf16[2,5,64,128]{3,2,1,0:T(8,128)(2,1)S(1)} %convolution_add_fusion.17) | copy-start | bytes 491524
  142.3 7.4 %copy-start.20 = (bf16[2,5,64,128]{3,2,1,0:T(8,128)(2,1)}, bf16[2,5,64,128]{3,2,1,0:T(8,128)(2,1)S(1)}, u32[]{:S(2)}) copy-start(bf16[2,5,64,128]{3,2,1,0:T(8,128)(2,1)S(1)} %convolution_add_fusion.16) | copy-start | bytes 491524
  143.7 6.0 %copy-start.22 = (bf16[2,5,64,128]{3,2,1,0:T(8,128)(2,1)}, bf16[2,5,64,128]{3,2,1,0:T(8,128)(2,1)S(1)}, u32[]{:S(2)}) copy-start(bf16[2,5,64,128]{3,2,1,0:T(8,128)(2,1)S(1)} %convolution_add_fusion.15) | copy-start | bytes 491524
  149.7 36.9 %all-to-all-start.2 = ((bf16[320,8,320]{0,2,1:T(8,128)(2,1)}), bf16[320,8,320]{0,2,1:T(8,128)(2,1)}, u32[]{:S(2)}, u32[]{:S(2)}) async-start(bf16[320,8,320]{0,2,1:T(8,128)(2,1)} %bitcast.219), calls=%async_computation.2 | async-start | bytes 3932160 | tf_op jit(solution)/shard_map/all_to_all | solution.py:210
  161.2 16.7 %copy-start.30 = (f32[2,5,64,128]{3,2,1,0:T(8,128)}, f32[2,5,64,128]{3,2,1,0:T(8,128)S(1)}, u32[]{:S(2)}) copy-start(f32[2,5,64,128]{3,2,1,0:T(8,128)S(1)} %convolution_add_fusion.13) | copy-start | bytes 983044
  180.1 3.0 %copy-start.5 = (f32[2,5,2,64,64]{3,4,2,1,0:T(8,128)S(1)}, f32[2,5,2,64,64]{3,4,2,1,0:T(8,128)}, u32[]{:S(2)}) copy-start(f32[2,5,2,64,64]{3,4,2,1,0:T(8,128)} %fusion.144) | copy-start | bytes 983044
  (25 other events, 41.5 us)
Sparse Core Ops, SparseCore 0:
  91.3 42.1 all-gather.4
  145.9 27.9 all-gather.6
